TPU v7x, 256 devices: a whole 4x4x8 slice. The times are simulated.
256 devices in a mesh: gx: 16 (over z, core), gy: 4 (over x), gz: 4 (over y).
Axes of the slice: x: 4, y: 4, z: 8, core: 2. Of those that a mesh axis runs over, the one named last changes fastest.
Arguments:
- block_values: bfloat16 [4, 64, 4, 6, 128, 128], P('gy', 'gx', 'gz'), as said below
- block_cols: int32 [4, 64, 4, 6], P('gy', 'gx', 'gz'), may hold values from 0 to 63, as said below
Outputs:
- purified: float32 [2048, 32768], P(('gx', 'gy'), 'gz')
Inputs may be any that keep to these rules, and one draw needn't show every extreme that they name: block_cols[a, s, b, :] holds 6 distinct tile columns of panel b at which tile row a * 64 + s of P is nonzero; every tile column of a panel is listed by exactly 6 tile rows of each slab; the pattern is symmetric: tile (i, j) is listed exactly when tile (j, i) is. `block_values`: P is symmetric: the tile listed at (i, j) is the transpose of the tile listed at (j, i), and diagonal tiles are symmetric.
All inputs are finite; a program needn't handle non-finite values.
Results may differ from a plain program's by a relative error of at most 0.0033.
Values may be sent and summed in bfloat16 or wider, within the bound.
A program may use at most 128 MiB of HBM per device.

v0:
```python
import jax
import jax.numpy as jnp
from jax import lax
from jax.sharding import PartitionSpec as P

WIN = 1


def picked_2(x, axis, root):
    return lax.dynamic_index_in_dim(lax.all_gather(x, axis), root, 0, keepdims=False)


def in_blocks(x, dim, length):
    lengths = x.shape
    tiles = x.reshape(*lengths[:dim], length, lengths[dim] // length, *lengths[dim + 1 :])
    return jnp.moveaxis(tiles, dim, 0)


def sent_and_summed(x, axis, dim):
    tiles = in_blocks(x, dim, lax.axis_size(axis))
    arrived = lax.all_to_all(tiles, axis, split_axis=0, concat_axis=0, tiled=True)
    return arrived.astype(jnp.float32).sum(axis=0)


def densify(left_tiles, left_columns, slab_tiles):
    onehot = (
        left_columns[:, :, None] == jnp.arange(slab_tiles, dtype=jnp.int32)[None, None, :]
    ).astype(jnp.bfloat16)
    densified = jnp.einsum("wkj,wkyx->wyjx", onehot, left_tiles, preferred_element_type=jnp.float32)
    tile_size = left_tiles.shape[2]
    return densified.astype(jnp.bfloat16).reshape(
        left_tiles.shape[0] * tile_size, slab_tiles, tile_size
    )


def product_one(left_panel, panel_tiles, panel_columns):
    summed = jnp.zeros(
        (left_panel.shape[0], panel_tiles.shape[0], panel_tiles.shape[2]), jnp.float32
    )
    for column_slot in range(panel_tiles.shape[1]):
        picked = jnp.take(left_panel, panel_columns[:, column_slot], axis=1)
        summed = summed + jnp.einsum(
            "rix,iyx->riy", picked, panel_tiles[:, column_slot], preferred_element_type=jnp.float32
        )
    return summed


def product_two(rounded, panel_tiles, panel_columns, panel_width):
    summed = jnp.zeros((rounded.shape[0], panel_width, panel_tiles.shape[3]), jnp.float32)
    for column_slot in range(panel_tiles.shape[1]):
        product = jnp.einsum(
            "rix,ixy->riy", rounded, panel_tiles[:, column_slot], preferred_element_type=jnp.float32
        )
        summed = summed.at[:, panel_columns[:, column_slot], :].add(product)
    return summed


def local(block_values, block_cols):
    tiles_here = block_values[0, :, 0]
    columns_here = block_cols[0, :, 0]
    tile_size = tiles_here.shape[2]
    slab_tiles = tiles_here.shape[0] * lax.axis_size("gx")
    left_tiles, left_columns = (
        picked_2(tiles_here[:WIN], "gy", 0),
        picked_2(columns_here[:WIN], "gy", 0),
    )
    left_panel = densify(left_tiles, left_columns, slab_tiles)
    height = left_panel.shape[0]
    on_diagonal = (lax.axis_index("gy") == lax.axis_index("gz")).astype(jnp.float32)
    panel_tiles, panel_columns = (
        lax.all_gather(tiles_here, "gx", axis=0, tiled=True),
        lax.all_gather(columns_here, "gx", axis=0, tiled=True),
    )
    partial_square = product_one(left_panel, panel_tiles, panel_columns)
    partial_square = partial_square.reshape(height, slab_tiles * tile_size)
    square = lax.psum(partial_square, "gz")
    square_low = square.astype(jnp.bfloat16).reshape(height, slab_tiles, tile_size)
    applied = product_two(square_low, panel_tiles, panel_columns, slab_tiles).reshape(
        height // lax.axis_size("gy") * lax.axis_size("gy"), slab_tiles * tile_size
    )
    return sent_and_summed(
        (3.0 * on_diagonal * square - 2.0 * applied).astype(jnp.bfloat16), "gy", 0
    )


def solution(mesh):
    in_specs = (P("gy", "gx", "gz", None, None, None), P("gy", "gx", "gz", None))
    out_specs = P(("gx", "gy"), "gz")
    return jax.shard_map(local, mesh=mesh, in_specs=in_specs, out_specs=out_specs, check_vma=False)
```

profile of v0, /device:TPU:32, one launch (start us, length us, event | category | flops | bytes accessed | tf_op | source)
XLA Modules:
  0.0 381.8 jit_solution(5912386459244780532)
XLA Ops:
  6.5 0.0 all-gather.6.cloned.1.call-start
  6.5 2.2 copy.30
  8.7 0.0 all-gather.6.cloned.1.call-update
  8.7 0.0 all-reduce.2.cloned.1.call-start
  8.8 9.7 %all-gather = s32[4,1,1,6]{3,2,1,0:T(1,128)S(1)} all-gather(s32[1,1,1,6]{3,2,1,0:T(1,128)S(1)} %slice-done.4), channel_id=2, replica_groups=mesh['gx'=16,'gy'=4,'gz'=4] {'gy'}, dimensions={0}, use_global_device_ids=true | all-gather | bytes 120 | tf_op jit(solution)/shard_map/all_gather | solution.py:10
  18.5 13.3 %all-gather.1 = bf16[4,1,1,6,128,128]{5,4,3,2,1,0:T(8,128)(2,1)S(1)} all-gather(bf16[1,1,1,6,128,128]{5,4,3,2,1,0:T(8,128)(2,1)S(1)} %slice-done.3), channel_id=3, replica_groups=mesh['gx'=16,'gy'=4,'gz'=4] {'gy'}, dimensions={0}, use_global_device_ids=true | all-gather | bytes 983040 | tf_op jit(solution)/shard_map/all_gather | solution.py:10
  31.8 0.8 convert_bitcast_fusion
  32.7 0.0 copy-start.5
  32.7 1.4 copy.29
  34.0 0.0 copy-done.5
  34.1 18.6 %all-gather.2 = s32[1,64,1,6]{3,2,0,1:T(1,128)S(1)} all-gather(s32[1,4,1,6]{3,2,0,1:T(1,128)S(1)} %bitcast.101), channel_id=4, replica_groups=mesh['gx'=16,'gy'=4,'gz'=4] {'gx'}, dimensions={1}, use_global_device_ids=true | all-gather | bytes 1632 | tf_op jit(solution)/shard_map/all_gather | solution.py:72
  52.7 0.4 fusion.41
  53.1 2.2 gather_fusion
  55.3 2.1 gather_fusion.4
  57.4 2.2 gather_fusion.3
  59.6 2.1 gather_fusion.2
  61.7 2.2 gather_fusion.1
  63.9 2.1 gather_fusion.5
  66.1 19.6 %all-gather.6.cloned.1.call-done = bf16[1,64,1,6,128,128]{5,4,1,3,2,0:T(8,128)(2,1)} async-done(((bf16[1,4,1,6,128,128]{5,4,1,3,2,0:T(8,128)(2,1)}), bf16[1,64,1,6,128,128]{5,4,1,3,2,0:T(8,128)(2,1)}) %all-gather.6.cloned.1.call-update) | async-done | bytes 12582928 | tf_op jit(solution)/shard_map/all_gather | solution.py:71
  85.7 6.2 %fusion.10 = f32[64,128,128]{1,2,0:T(8,128)} fusion(bf16[64,128,128]{2,1,0:T(8,128)(2,1)} %gather_fusion, pred[64]{0:T(512)(128)(4,1)S(1)} %get-tuple-element.29, bf16[64,6,128,128]{3,2,0,1:T(8,128)(2,1)} %bitcast.84), kind=kOutput, calls=%fused_computation.31 | convolution fusion | flops 269484032 | bytes 8388672 | tf_op jit(solution)/shard_map/rix,iyx->riy/dot_general | solution.py:42
  91.8 6.0 %fusion.2 = f32[64,128,128]{1,2,0:T(8,128)} fusion(bf16[64,128,128]{2,1,0:T(8,128)(2,1)} %gather_fusion.4, pred[64]{0:T(512)(128)(4,1)S(1)} %get-tuple-element.25, bf16[64,6,128,128]{3,2,0,1:T(8,128)(2,1)} %bitcast.85), kind=kOutput, calls=%fused_computation.23 | convolution fusion | flops 269484032 | bytes 8388672 | tf_op jit(solution)/shard_map/rix,iyx->riy/dot_general | solution.py:42
  97.8 3.6 fusion.4
  101.5 3.6 fusion.6
  105.1 3.6 fusion.8
  108.7 10.1 %add_add_fusion = f32[64,128,128]{1,2,0:T(8,128)} fusion(f32[64,128,128]{1,2,0:T(8,128)} %fusion.2, f32[64,128,128]{1,2,0:T(8,128)} %fusion.4, f32[64,128,128]{1,2,0:T(8,128)} %fusion.6, f32[64,128,128]{1,2,0:T(8,128)} %fusion.10, f32[64,128,128]{1,2,0:T(8,128)} %fusion.8, bf16[64,128,128]{2,1,0:T(8,128)(2,1)S(1)} %copy-done.4, ...), kind=kOutput, calls=%fused_computation.15 | convolution fusion | flops 274726912 | bytes 29360640 | tf_op jit(solution)/shard_map/rix,iyx->riy/dot_general | solution.py:42
  118.8 0.0 all-reduce.2.cloned.1.call-update
  118.8 98.5 %all-reduce.2.cloned.1.call-done = f32[128,8192]{0,1:T(8,128)} async-done(((f32[128,8192]{0,1:T(8,128)}), f32[128,8192]{0,1:T(8,128)}) %all-reduce.2.cloned.1.call-update) | async-done | bytes 4194320 | tf_op jit(solution)/shard_map/psum | solution.py:76
  217.4 2.5 convert_element_type.27
  219.9 0.0 slice-start.1
  219.9 4.6 %fusion.24 = f32[64,128,128]{2,1,0:T(8,128)} fusion(bf16[128,64,128]{0,2,1:T(8,128)(2,1)S(1)} %bitcast.78, bf16[64,6,128,128]{3,2,0,1:T(8,128)(2,1)} %bitcast.86), kind=kOutput, calls=%fused_computation.47 | convolution fusion | flops 268435456 | bytes 8388608 | tf_op jit(solution)/shard_map/rix,ixy->riy/dot_general | solution.py:51
  224.5 4.6 %fusion.25 = f32[64,128,128]{2,1,0:T(8,128)} fusion(bf16[128,64,128]{0,2,1:T(8,128)(2,1)S(1)} %bitcast.79, bf16[64,6,128,128]{3,2,0,1:T(8,128)(2,1)} %bitcast.87), kind=kOutput, calls=%fused_computation.48 | convolution fusion | flops 268435456 | bytes 8388608 | tf_op jit(solution)/shard_map/rix,ixy->riy/dot_general | solution.py:51
  229.1 2.8 fusion.26
  231.9 2.8 fusion.27
  234.7 2.8 fusion.28
  237.5 2.8 fusion.29
  240.3 2.5 broadcast_in_dim.11
  242.8 13.7 %scatter_fusion = f32[128,64,128]{2,0,1:T(8,128)} fusion(f32[128,64,128]{2,0,1:T(8,128)} %broadcast_in_dim.11, s32[64]{0:T(128)S(1)} %get-tuple-element.7, f32[64,128,128]{2,1,0:T(8,128)} %fusion.24), kind=kCustom, calls=%fused_computation.6 | custom fusion | flops 1048576 | bytes 12583168 | tf_op jit(solution)/shard_map/scatter-add | solution.py:54
  256.5 13.7 %scatter_fusion.1 = f32[128,64,128]{2,0,1:T(8,128)} fusion(f32[128,64,128]{2,0,1:T(8,128)} %scatter_fusion, s32[64]{0:T(128)S(1)} %get-tuple-element.8, f32[64,128,128]{2,1,0:T(8,128)} %fusion.25), kind=kCustom, calls=%fused_computation.7 | custom fusion | flops 1048576 | bytes 12583168 | tf_op jit(solution)/shard_map/scatter-add | solution.py:54
  270.2 13.7 %scatter_fusion.2 = f32[128,64,128]{2,0,1:T(8,128)} fusion(f32[128,64,128]{2,0,1:T(8,128)} %scatter_fusion.1, s32[64]{0:T(128)S(1)} %get-tuple-element.9, f32[64,128,128]{2,1,0:T(8,128)} %fusion.26), kind=kCustom, calls=%fused_computation.8 | custom fusion | flops 1048576 | bytes 12583168 | tf_op jit(solution)/shard_map/scatter-add | solution.py:54
  283.9 13.6 %scatter_fusion.3 = f32[128,64,128]{2,0,1:T(8,128)} fusion(f32[128,64,128]{2,0,1:T(8,128)} %scatter_fusion.2, s32[64]{0:T(128)S(1)} %get-tuple-element.10, f32[64,128,128]{2,1,0:T(8,128)} %fusion.27), kind=kCustom, calls=%fused_computation.9 | custom fusion | flops 1048576 | bytes 12583168 | tf_op jit(solution)/shard_map/scatter-add | solution.py:54
  297.5 13.7 %scatter_fusion.4 = f32[128,64,128]{2,0,1:T(8,128)} fusion(f32[128,64,128]{2,0,1:T(8,128)} %scatter_fusion.3, s32[64]{0:T(128)S(1)} %get-tuple-element.11, f32[64,128,128]{2,1,0:T(8,128)} %fusion.28), kind=kCustom, calls=%fused_computation.10 | custom fusion | flops 1048576 | bytes 12583168 | tf_op jit(solution)/shard_map/scatter-add | solution.py:54
  311.1 13.6 %scatter_fusion.5 = f32[128,64,128]{2,0,1:T(8,128)} fusion(f32[128,64,128]{2,0,1:T(8,128)} %scatter_fusion.4, s32[64]{0:T(128)S(1)} %get-tuple-element.6, f32[64,128,128]{2,1,0:T(8,128)} %fusion.29), kind=kCustom, calls=%fused_computation.11 | custom fusion | flops 1048576 | bytes 12583168 | tf_op jit(solution)/shard_map/scatter-add | solution.py:54
  324.8 4.7 %broadcast_multiply_fusion = f32[128,64,128]{2,0,1:T(8,128)} fusion(f32[128,64,128]{2,0,1:T(8,128)} %scatter_fusion.5), kind=kLoop, calls=%fused_computation.39 | loop fusion | flops 1048576 | bytes 8388608 | tf_op jit(solution)/shard_map/mul | solution.py:82
  329.5 5.6 %copy.42 = f32[128,64,128]{0,2,1:T(8,128)} copy(f32[128,64,128]{2,0,1:T(8,128)} %broadcast_multiply_fusion) | data formatting | bytes 8388608 | tf_op jit(solution)/shard_map/mul | solution.py:82
  335.1 5.2 %fusion = bf16[128,8192]{0,1:T(8,128)(2,1)} fusion(f32[128,64,128]{0,2,1:T(8,128)} %copy.42, f32[128,8192]{0,1:T(8,128)} %all-reduce.2.cloned.1.call-done, f32[]{:T(128)S(6)} %mul_shard_map.3), kind=kLoop, calls=%fused_computation.13 | loop fusion | flops 3145728 | bytes 10485764 | tf_op jit(solution)/shard_map/convert_element_type | solution.py:82
  340.3 2.9 copy.43
  343.3 30.4 %all_to_all.5 = bf16[4,32,8192]{2,1,0:T(8,128)(2,1)S(1)} all-to-all(bf16[4,32,8192]{2,1,0:T(8,128)(2,1)S(1)} %bitcast.99), channel_id=1, replica_groups=mesh['gx'=16,'gy'=4,'gz'=4] {'gy'}, dimensions={0} | all-to-all | bytes 4194304 | tf_op jit(solution)/shard_map/all_to_all | solution.py:21
  373.6 1.3 convert_reduce_fusion
  (34 shorter events, 0.1 us)
Async XLA Ops:
  6.5 12.0 %slice-start.3 = ((bf16[1,4,1,6,128,128]{5,4,3,2,1,0:T(8,128)(2,1)}), bf16[1,1,1,6,128,128]{5,4,3,2,1,0:T(8,128)(2,1)S(1)}, s32[]{:S(2)}) async-start(bf16[1,4,1,6,128,128]{5,4,3,2,1,0:T(8,128)(2,1)} %param.4), calls=%async_computation.6 | async-start | bytes 393216 | tf_op jit(solution)/shard_map/slice | solution.py:64
  6.5 2.2 slice-start.4
  6.5 79.1 %all-gather.6.cloned.1.call-start = ((), (), s32[]{:S(2)}) async-start(), calls=%async_computation.2 | async-start | bytes 13369344 | tf_op jit(solution)/shard_map/all_gather | solution.py:71
  8.7 208.6 %all-reduce.2.cloned.1.call-start = ((), (), s32[]{:S(2)}) async-start(), calls=%async_computation.1 | async-start | bytes 8388608 | tf_op jit(solution)/shard_map/psum | solution.py:76
  32.7 1.4 copy-start.5
  85.7 12.2 %copy-start = (bf16[1,64,1,6,128,128]{5,4,1,3,2,0:T(8,128)(2,1)S(1)}, bf16[1,64,1,6,128,128]{5,4,1,3,2,0:T(8,128)(2,1)}, u32[]{:S(2)}) copy-start(bf16[1,64,1,6,128,128]{5,4,1,3,2,0:T(8,128)(2,1)} %all-gather.6.cloned.1.call-done) | copy-start | bytes 37748740
  91.8 6.0 %copy-start.1 = (bf16[64,128,128]{2,1,0:T(8,128)(2,1)S(1)}, bf16[64,128,128]{2,1,0:T(8,128)(2,1)}, u32[]{:S(2)}) copy-start(bf16[64,128,128]{2,1,0:T(8,128)(2,1)} %gather_fusion.3) | copy-start | bytes 6291460
  97.8 3.6 copy-start.2
  101.5 3.6 copy-start.3
  105.1 3.6 copy-start.4
  217.4 11.7 %slice-start = ((s8[12582912]{0:T(1024)(128)(4,1)}), s8[4194304]{0:T(1024)(128)(4,1)S(1)}, s32[]{:S(2)}) async-start(s8[12582912]{0:T(1024)(128)(4,1)} %bitcast.92), calls=%async_computation.3 | async-start | bytes 8388608
  219.9 9.2 %slice-start.1 = ((s8[12582912]{0:T(1024)(128)(4,1)}), s8[4194304]{0:T(1024)(128)(4,1)S(1)}, s32[]{:S(2)}) async-start(s8[12582912]{0:T(1024)(128)(4,1)} %bitcast.92), calls=%async_computation.4 | async-start | bytes 8388608
  224.5 4.6 %slice-start.2 = ((s8[12582912]{0:T(1024)(128)(4,1)}), s8[4194304]{0:T(1024)(128)(4,1)S(1)}, s32[]{:S(2)}) async-start(s8[12582912]{0:T(1024)(128)(4,1)} %bitcast.92), calls=%async_computation.5 | async-start | bytes 8388608
Sparse Core Ops, SparseCore 0:
  9.2 76.4 all-gather.5
  118.9 98.3 all-reduce.1
where the time goes:
time: 383 us; the launch traced here: 382 us
  waiting for transfers between devices  118 us (31%)
  other arithmetic  96.3 us (25%)
  blocking collectives  72 us (19%)
  matrix products  54.3 us (14%)
  local copies, waits for them, and re-layouts  27.4 us (7%)
  between operations  13.5 us (4%)
    psum x1, waiting for transfers between devices, local(): square = lax.psum(partial_square, 'gz')  98.5 us
    scatter-add x6, other arithmetic, product_two(): summed = summed.at[:, panel_columns[:, column_slot], :].add(product)  82 us
    dot_general x6, matrix products, product_one(): jnp.einsum('rix,iyx->riy', picked, panel_tiles[:, column_slot], preferred...  33.1 us
    all_to_all x1, blocking collectives, sent_and_summed(): lax.all_to_all(tiles, axis, split_axis=0, concat_axis=0, tiled=True)  30.4 us
    all_gather x2, blocking collectives, picked_2(): lax.all_gather(x, axis)  23 us
    dot_general x6, matrix products, product_two(): jnp.einsum('rix,ixy->riy', rounded, panel_tiles[:, column_slot], preferre...  20.4 us
    all_gather x1, waiting for transfers between devices, local(): lax.all_gather(tiles_here, 'gx', axis=0, tiled=True)  19.6 us
    all_gather x1, blocking collectives, local(): lax.all_gather(columns_here, 'gx', axis=0, tiled=True)  18.6 us
  transfers between devices with their start and end apart: 2, of which 2 were waited for; matrix products, arithmetic and copies ran while one was open for 4% of the time, Pallas kernels for 0%

commit v1 on v0

--- a/solution.py
+++ b/solution.py
@@ -68,7 +68,9 @@
     height = left_panel.shape[0]
     on_diagonal = (lax.axis_index("gy") == lax.axis_index("gz")).astype(jnp.float32)
     panel_tiles, panel_columns = (
-        lax.all_gather(tiles_here, "gx", axis=0, tiled=True),
+        jnp.concatenate(
+            lax.all_to_all(jnp.stack([tiles_here] * lax.axis_size("gx")), "gx", 0, 0), axis=0
+        ),
         lax.all_gather(columns_here, "gx", axis=0, tiled=True),
     )
     partial_square = product_one(left_panel, panel_tiles, panel_columns)

time: 383 us -> 619 us (1.62)
  blocking collectives: 72 us -> 310 us
  waiting for transfers between devices: 118 us -> 99.3 us
  local copies, waits for them, and re-layouts: 27.4 us -> 41.7 us
  starting transfers between devices: 0.04 us -> 8.76 us
  matrix products: 54.3 us -> 47.9 us
    all_gather x1, blocking collectives: 18.6 us -> 256 us  [local(): lax.all_gather(columns_here, 'gx', axis=0, tiled=True)]
    all_gather x1 -> x0, waiting for transfers between devices: 19.6 us -> none  [local(): lax.all_gather(tiles_here, 'gx', axis=0, tiled=True)]
    another operation x0 -> x2, local copies, waits for them, and re-layouts: none -> 8.86 us  [local(): jnp.stack([tiles_here] * lax.axis_size('gx'))]
    all_to_all x0 -> x1, starting transfers between devices: none -> 8.72 us  [local(): lax.all_to_all(jnp.stack([tiles_here] * lax.axis_size('gx')), 'gx', 0, 0)]
    all_to_all x0 -> x1, local copies, waits for them, and re-layouts: none -> 6.63 us  [local(): lax.all_to_all(jnp.stack([tiles_here] * lax.axis_size('gx')), 'gx', 0, 0)]
  transfers between devices with their start and end apart: 2 -> 2, of which waited for: 2 -> 1; matrix products, arithmetic and copies ran while one was open for 4% -> 3% of each run, Pallas kernels for 0% -> 0%
where the time goes in v1:
time: 619 us; the launch traced here: 618 us
  blocking collectives  310 us (50%)
  waiting for transfers between devices  99.3 us (16%)
  other arithmetic  96.3 us (16%)
  matrix products  47.9 us (8%)
  local copies, waits for them, and re-layouts  41.7 us (7%)
  between operations  13.6 us (2%)
  starting transfers between devices  8.76 us (1%)
    all_gather x1, blocking collectives, local(): lax.all_gather(columns_here, 'gx', axis=0, tiled=True)  256 us
    psum x1, waiting for transfers between devices, local(): square = lax.psum(partial_square, 'gz')  99.3 us
    scatter-add x6, other arithmetic, product_two(): summed = summed.at[:, panel_columns[:, column_slot], :].add(product)  82 us
    all_to_all x1, blocking collectives, sent_and_summed(): lax.all_to_all(tiles, axis, split_axis=0, concat_axis=0, tiled=True)  30.4 us
    dot_general x6, matrix products, product_one(): jnp.einsum('rix,iyx->riy', picked, panel_tiles[:, column_slot], preferred...  28.3 us
    all_gather x2, blocking collectives, picked_2(): lax.all_gather(x, axis)  23.7 us
    dot_general x6, matrix products, product_two(): jnp.einsum('rix,ixy->riy', rounded, panel_tiles[:, column_slot], preferre...  18.8 us
    gather x6, local copies, waits for them, and re-layouts, product_one(): picked = jnp.take(left_panel, panel_columns[:, column_slot], axis=1)  12.9 us
  transfers between devices with their start and end apart: 2, of which 1 were waited for; matrix products, arithmetic and copies ran while one was open for 3% of the time, Pallas kernels for 0%

profile of v1, /device:TPU:32, one launch (start us, length us, event | category | flops | bytes accessed | tf_op | source)
XLA Modules:
  0.0 617.6 jit_solution(18401325591720764018)
XLA Ops:
  6.5 1.2 copy.30
  7.7 7.7 %stack.3 = bf16[16,4,6,128,128]{4,3,1,2,0:T(8,128)(2,1)} broadcast(bf16[4,6,128,128]{3,2,0,1:T(8,128)(2,1)S(1)} %copy.30), dimensions={1,2,3,4} | broadcast | bytes 13369344 | tf_op jit(solution)/shard_map/stack | solution.py:72
  15.4 8.7 %all-to-all-start = ((bf16[16,4,6,128,128]{4,3,1,2,0:T(8,128)(2,1)}), bf16[16,4,6,128,128]{4,3,1,2,0:T(8,128)(2,1)}, u32[]{:S(2)}, u32[]{:S(2)}) async-start(bf16[16,4,6,128,128]{4,3,1,2,0:T(8,128)(2,1)} %stack.3), calls=%async_computation | async-start | bytes 25165824 | tf_op jit(solution)/shard_map/all_to_all | solution.py:72
  24.1 0.0 all-reduce.2.cloned.1.call-start
  24.2 9.7 %all-gather = s32[4,1,1,6]{3,2,1,0:T(1,128)S(1)} all-gather(s32[1,1,1,6]{3,2,1,0:T(1,128)S(1)} %slice-done), channel_id=2, replica_groups=mesh['gx'=16,'gy'=4,'gz'=4] {'gy'}, dimensions={0}, use_global_device_ids=true | all-gather | bytes 120 | tf_op jit(solution)/shard_map/all_gather | solution.py:10
  33.9 0.9 slice.59
  34.8 13.9 %all-gather.1 = bf16[4,1,1,6,128,128]{5,4,3,2,1,0:T(8,128)(2,1)S(1)} all-gather(bf16[1,1,1,6,128,128]{5,4,3,2,1,0:T(8,128)(2,1)S(1)} %slice.59), channel_id=3, replica_groups=mesh['gx'=16,'gy'=4,'gz'=4] {'gy'}, dimensions={0}, use_global_device_ids=true | all-gather | bytes 983040 | tf_op jit(solution)/shard_map/all_gather | solution.py:10
  48.8 0.8 convert_bitcast_fusion
  49.6 1.4 copy.29
  51.0 256.0 %all-gather.2 = s32[1,64,1,6]{3,2,0,1:T(1,128)S(1)} all-gather(s32[1,4,1,6]{3,2,0,1:T(1,128)S(1)} %bitcast.101), channel_id=4, replica_groups=mesh['gx'=16,'gy'=4,'gz'=4] {'gx'}, dimensions={1}, use_global_device_ids=true | all-gather | bytes 1632 | tf_op jit(solution)/shard_map/all_gather | solution.py:74
  307.0 0.4 fusion.41
  307.5 2.2 gather_fusion.4
  309.7 2.1 gather_fusion.3
  311.8 2.2 gather_fusion.2
  314.0 2.1 gather_fusion
  316.1 2.2 gather_fusion.1
  318.3 2.1 gather_fusion.5
  320.5 0.0 all-to-all-done
  320.5 6.6 %copy.31 = bf16[16,4,6,128,128]{4,3,1,0,2:T(8,128)(2,1)S(1)} copy(bf16[16,4,6,128,128]{4,3,1,2,0:T(8,128)(2,1)} %all-to-all-done) | data formatting | bytes 25165824 | tf_op jit(solution)/shard_map/all_to_all | solution.py:72
  327.1 0.0 copy-start
  327.2 3.6 fusion.2
  330.8 3.8 fusion.4
  334.5 3.6 fusion.6
  338.2 3.6 fusion.10
  341.8 3.6 fusion.8
  345.4 10.1 %add_add_fusion = f32[64,128,128]{1,2,0:T(8,128)} fusion(f32[64,128,128]{1,2,0:T(8,128)} %fusion.2, f32[64,128,128]{1,2,0:T(8,128)} %fusion.4, f32[64,128,128]{1,2,0:T(8,128)} %fusion.6, f32[64,128,128]{1,2,0:T(8,128)} %fusion.10, f32[64,128,128]{1,2,0:T(8,128)} %fusion.8, bf16[64,128,128]{2,1,0:T(8,128)(2,1)S(1)} %copy-done.7, ...), kind=kOutput, calls=%fused_computation.15 | convolution fusion | flops 274726912 | bytes 29360640 | tf_op jit(solution)/shard_map/rix,iyx->riy/dot_general | solution.py:42
  355.5 0.0 all-reduce.2.cloned.1.call-update
  355.5 99.3 %all-reduce.2.cloned.1.call-done = f32[128,8192]{0,1:T(8,128)} async-done(((f32[128,8192]{0,1:T(8,128)}), f32[128,8192]{0,1:T(8,128)}) %all-reduce.2.cloned.1.call-update) | async-done | bytes 4194320 | tf_op jit(solution)/shard_map/psum | solution.py:78
  454.8 2.5 convert_element_type.27
  457.4 4.7 fusion.24
  462.1 2.8 fusion.25
  464.9 2.8 fusion.26
  467.7 2.8 fusion.27
  470.6 2.8 fusion.28
  473.4 2.8 fusion.29
  476.2 2.5 broadcast_in_dim.11
  478.6 13.7 %scatter_fusion = f32[128,64,128]{2,0,1:T(8,128)} fusion(f32[128,64,128]{2,0,1:T(8,128)} %broadcast_in_dim.11, s32[64]{0:T(128)S(1)} %get-tuple-element.7, f32[64,128,128]{2,1,0:T(8,128)} %fusion.24), kind=kCustom, calls=%fused_computation.6 | custom fusion | flops 1048576 | bytes 12583168 | tf_op jit(solution)/shard_map/scatter-add | solution.py:54
  492.3 13.7 %scatter_fusion.1 = f32[128,64,128]{2,0,1:T(8,128)} fusion(f32[128,64,128]{2,0,1:T(8,128)} %scatter_fusion, s32[64]{0:T(128)S(1)} %get-tuple-element.8, f32[64,128,128]{2,1,0:T(8,128)} %fusion.25), kind=kCustom, calls=%fused_computation.7 | custom fusion | flops 1048576 | bytes 12583168 | tf_op jit(solution)/shard_map/scatter-add | solution.py:54
  506.1 13.7 %scatter_fusion.2 = f32[128,64,128]{2,0,1:T(8,128)} fusion(f32[128,64,128]{2,0,1:T(8,128)} %scatter_fusion.1, s32[64]{0:T(128)S(1)} %get-tuple-element.9, f32[64,128,128]{2,1,0:T(8,128)} %fusion.26), kind=kCustom, calls=%fused_computation.8 | custom fusion | flops 1048576 | bytes 12583168 | tf_op jit(solution)/shard_map/scatter-add | solution.py:54
  519.8 13.6 %scatter_fusion.3 = f32[128,64,128]{2,0,1:T(8,128)} fusion(f32[128,64,128]{2,0,1:T(8,128)} %scatter_fusion.2, s32[64]{0:T(128)S(1)} %get-tuple-element.10, f32[64,128,128]{2,1,0:T(8,128)} %fusion.27), kind=kCustom, calls=%fused_computation.9 | custom fusion | flops 1048576 | bytes 12583168 | tf_op jit(solution)/shard_map/scatter-add | solution.py:54
  533.3 13.7 %scatter_fusion.4 = f32[128,64,128]{2,0,1:T(8,128)} fusion(f32[128,64,128]{2,0,1:T(8,128)} %scatter_fusion.3, s32[64]{0:T(128)S(1)} %get-tuple-element.11, f32[64,128,128]{2,1,0:T(8,128)} %fusion.28), kind=kCustom, calls=%fused_computation.10 | custom fusion | flops 1048576 | bytes 12583168 | tf_op jit(solution)/shard_map/scatter-add | solution.py:54
  547.0 13.6 %scatter_fusion.5 = f32[128,64,128]{2,0,1:T(8,128)} fusion(f32[128,64,128]{2,0,1:T(8,128)} %scatter_fusion.4, s32[64]{0:T(128)S(1)} %get-tuple-element.6, f32[64,128,128]{2,1,0:T(8,128)} %fusion.29), kind=kCustom, calls=%fused_computation.11 | custom fusion | flops 1048576 | bytes 12583168 | tf_op jit(solution)/shard_map/scatter-add | solution.py:54
  560.6 4.7 broadcast_multiply_fusion
  565.4 5.6 copy.43
  571.0 5.2 fusion
  576.2 2.9 copy.44
  579.1 30.4 %all_to_all.10 = bf16[4,32,8192]{2,1,0:T(8,128)(2,1)S(1)} all-to-all(bf16[4,32,8192]{2,1,0:T(8,128)(2,1)S(1)} %bitcast.98), channel_id=1, replica_groups=mesh['gx'=16,'gy'=4,'gz'=4] {'gy'}, dimensions={0} | all-to-all | bytes 4194304 | tf_op jit(solution)/shard_map/all_to_all | solution.py:21
  609.5 1.3 convert_reduce_fusion
  (33 shorter events, 0.1 us)
Async XLA Ops:
  15.4 8.8 %slice-start = ((s32[1,4,1,6]{3,2,1,0:T(1,128)}), s32[1,1,1,6]{3,2,1,0:T(1,128)S(1)}, s32[]{:S(2)}) async-start(s32[1,4,1,6]{3,2,1,0:T(1,128)} %param.5), calls=%async_computation.3 | async-start | bytes 1024 | tf_op jit(solution)/shard_map/slice | solution.py:65
  15.4 305.1 %all-to-all-start = ((bf16[16,4,6,128,128]{4,3,1,2,0:T(8,128)(2,1)}), bf16[16,4,6,128,128]{4,3,1,2,0:T(8,128)(2,1)}, u32[]{:S(2)}, u32[]{:S(2)}) async-start(bf16[16,4,6,128,128]{4,3,1,2,0:T(8,128)(2,1)} %stack.3), calls=%async_computation | async-start | bytes 25165824 | tf_op jit(solution)/shard_map/all_to_all | solution.py:72
  24.1 26.9 %copy-start.8 = (s32[1,4,1,6]{3,2,1,0:T(1,128)S(1)}, s32[1,4,1,6]{3,2,1,0:T(1,128)}, u32[]{:S(2)}) copy-start(s32[1,4,1,6]{3,2,1,0:T(1,128)} %param.5) | copy-start | bytes 292
  24.1 430.7 %all-reduce.2.cloned.1.call-start = ((), (), s32[]{:S(2)}) async-start(), calls=%async_computation.2 | async-start | bytes 8388608 | tf_op jit(solution)/shard_map/psum | solution.py:78
  320.5 6.7 %copy-start.2 = (bf16[64,128,128]{2,1,0:T(8,128)(2,1)S(1)}, bf16[64,128,128]{2,1,0:T(8,128)(2,1)}, u32[]{:S(2)}) copy-start(bf16[64,128,128]{2,1,0:T(8,128)(2,1)} %gather_fusion.4) | copy-start | bytes 6291460
  327.1 18.2 %copy-start = (bf16[16,4,6,128,128]{4,3,1,0,2:T(8,128)(2,1)}, bf16[16,4,6,128,128]{4,3,1,0,2:T(8,128)(2,1)S(1)}, u32[]{:S(2)}) copy-start(bf16[16,4,6,128,128]{4,3,1,0,2:T(8,128)(2,1)S(1)} %copy.31) | copy-start | bytes 37748740
  327.2 3.6 copy-start.3
  330.8 3.8 copy-start.4
  334.5 3.6 copy-start.5
  338.2 3.6 copy-start.6
  341.8 3.6 copy-start.7
  454.8 7.3 %copy-start.1 = (bf16[16,4,6,128,128]{4,3,1,0,2:T(8,128)(2,1)S(1)}, bf16[16,4,6,128,128]{4,3,1,0,2:T(8,128)(2,1)}, u32[]{:S(2)}) copy-start(bf16[16,4,6,128,128]{4,3,1,0,2:T(8,128)(2,1)} %copy-done) | copy-start | bytes 37748740
Sparse Core Ops, SparseCore 0:
  355.7 99.1 all-reduce.1
